TPU v7x, 32 devices: a whole 2x2x4 slice. The times are simulated.
32 devices in a mesh: rows: 8 (over z, y), sub: 4 (over x, core).
Axes of the slice: x: 2, y: 2, z: 4, core: 2. Of those that a mesh axis runs over, the one named last changes fastest.
Arguments:
- frames: float32 [15, 32768], P(None, ('rows', 'sub')), may hold values from -1 to 1, as said below
- start_vector: float32 [3, 32768], P(None, ('rows', 'sub')), may hold values from -12 to 12
- edge_blocks: float32 [36, 65536], P(None, ('rows', 'sub')), may hold values from -14.4 to 14.4
- edge_source: int32 [32, 2048], P(('rows', 'sub')), may hold values from 0 to 1023
- edge_target: int32 [32, 2048], P(('rows', 'sub')), may hold values from 0 to 1535, as said below
- edge_count: int32 [32], P(('rows', 'sub')), may hold values from 1024 to 2048, as said below
- send_index: int32 [32, 512], P(('rows', 'sub')), may hold values from 0 to 1024, as said below
Outputs:
- new_frames: float32 [15, 32768], P(None, ('rows', 'sub'))
- last_vector: float32 [3, 32768], P(None, ('rows', 'sub'))
- tridiagonal: float32 [2, 4], replicated
Inputs may be any that keep to these rules, and one draw needn't show every extreme that they name: `frames`: each pose's block has orthonormal columns to float32 rounding. `edge_target`: below 1024: a pose of the same device. 1024 + u: halo slot u, whose block u // 16 on the providing device is never empty. `edge_count`: some device uses all 2048 slots. `send_index`: row q holds, in blocks of 16, the local poses that device q provides to device p (block p); a block is all poses or all 1024, which marks it empty; a device's block for itself is empty.
All inputs are finite; a program needn't handle non-finite values.
Results may differ from a plain program's by a relative error of at most 0.0003.
Values sent between devices are 32-bit elements; how exact they have to be, the bound alone decides.
A program may use at most 64 MiB of HBM per device.

v0:
```python
import jax
import jax.numpy as jnp
from jax import lax
from jax.sharding import PartitionSpec as P

RANK = 5
DIM = 3
LANCZOS = 4
polar_steps = 8
step_length = 0.3
epsilon = 1e-06


def symmetric(edge_blocks):
    blocks_six = edge_blocks.reshape(6, 6, -1)
    return 0.5 * (blocks_six + blocks_six.transpose(1, 0, 2))


def block_product(matrix, field_in):
    return jnp.sum(matrix[None, :, :, :] * field_in[:, None, :, :], axis=2)


def multiplier(left_field, right_field):
    product = jnp.sum(left_field[:, :, None, :] * right_field[:, None, :, :], axis=0)
    return 0.5 * (product + product.transpose(1, 0, 2))


def right_product(field_in, matrix):
    return jnp.sum(field_in[:, :, None, :] * matrix[None, :, :, :], axis=1)


def take_columns(table, index):
    return jnp.take(table, index, axis=1, mode="fill", fill_value=0.0)


def add_columns(values, index, width):
    total = jnp.zeros((values.shape[0], width), jnp.float32)
    return total.at[:, index].add(values, mode="drop")


def pack_rows(field_in, send_row):
    flattened = field_in.reshape(-1, field_in.shape[-1])
    return take_columns(flattened, send_row)


def return_rows(returned, send_row, poses_here):
    return add_columns(returned, send_row, poses_here)


def edge_terms(field_in, halo_vals, coupling, source, target, weight):
    copies = field_in.shape[0]
    poses_here = field_in.shape[2]
    edge_total = source.shape[0]
    extended = jnp.concatenate([field_in, halo_vals.reshape(copies, DIM, -1)], axis=2)
    full_width = extended.shape[2]
    values_first = take_columns(field_in.reshape(copies * DIM, poses_here), source).reshape(
        copies, DIM, edge_total
    )
    values_second = take_columns(extended.reshape(copies * DIM, full_width), target).reshape(
        copies, DIM, edge_total
    )
    upper_part = block_product(coupling[:3, :3], values_first) + block_product(
        coupling[:3, 3:], values_second
    )
    lower_part = block_product(coupling[3:, :3], values_first) + block_product(
        coupling[3:, 3:], values_second
    )
    upper_sum = add_columns(
        (upper_part * weight).reshape(copies * DIM, edge_total), source, poses_here
    )
    lower_sum = add_columns(
        (lower_part * weight).reshape(copies * DIM, edge_total), target, full_width
    )
    home_part = (upper_sum + lower_sum[:, :poses_here]).reshape(copies, DIM, poses_here)
    far_part = lower_sum[:, poses_here:].reshape(copies, DIM, full_width - poses_here)
    return (home_part, far_part)


def retract(frame_now, gradient, length):
    moved = frame_now - length * gradient
    norms = jnp.sum(moved * moved, axis=(0, 1))
    polar_now = moved * jnp.sqrt(DIM / norms)[None, None, :]
    identity = jnp.eye(DIM, dtype=jnp.float32)[:, :, None]
    for iteration in range(polar_steps):
        gram_matrix = jnp.sum(polar_now[:, :, None, :] * polar_now[:, None, :, :], axis=0)
        polar_now = right_product(polar_now, 1.5 * identity - 0.5 * gram_matrix)
    return polar_now


def on_device(frames, start_vector, edge_blocks, edge_source, edge_target, edge_count, send_index):
    poses_here = frames.shape[1]
    shards = lax.axis_size("rows") * lax.axis_size("sub")
    coupling = symmetric(edge_blocks)
    source = edge_source[0]
    target = edge_target[0]
    send_row = send_index[0]
    weight = (jnp.arange(source.shape[0], dtype=jnp.int32) < edge_count[0]).astype(jnp.float32)

    def split_product(field_in, halo_vals):
        return edge_terms(field_in, halo_vals, coupling, source, target, weight)

    frame_now = frames.reshape(RANK, DIM, poses_here)
    halo_vals = lax.all_to_all(
        pack_rows(frame_now, send_row), ("rows", "sub"), split_axis=1, concat_axis=1, tiled=True
    )
    near_part, far_part = split_product(frame_now, halo_vals)
    returned = lax.all_to_all(
        far_part.reshape(RANK * DIM, -1), ("rows", "sub"), split_axis=1, concat_axis=1, tiled=True
    )
    euclidean = near_part + return_rows(returned, send_row, poses_here).reshape(
        RANK, DIM, poses_here
    )
    multipliers = multiplier(frame_now, euclidean)
    gradient = 2.0 * (euclidean - right_product(frame_now, multipliers))
    total_square = lax.psum(jnp.sum(gradient * gradient), ("rows", "sub"))
    length = (
        step_length * jnp.sqrt(jnp.float32(poses_here * shards)) / jnp.sqrt(total_square + epsilon)
    )
    retracted = retract(frame_now, gradient, length)
    halo_moved = lax.all_to_all(
        pack_rows(retracted, send_row), ("rows", "sub"), split_axis=1, concat_axis=1, tiled=True
    )
    near_moved, far_moved = split_product(retracted, halo_moved)
    returned_moved = lax.all_to_all(
        far_moved.reshape(RANK * DIM, -1), ("rows", "sub"), split_axis=1, concat_axis=1, tiled=True
    )
    product_new = near_moved + return_rows(returned_moved, send_row, poses_here).reshape(
        RANK, DIM, poses_here
    )
    certificate_mult = multiplier(retracted, product_new)
    entries = DIM * poses_here * shards
    start_square = lax.psum(jnp.sum(start_vector * start_vector), ("rows", "sub"))
    start_field = start_vector.reshape(1, DIM, poses_here)
    krylov_basis = [start_field / jnp.sqrt(start_square / entries + epsilon)]
    alpha_list = []
    beta_list = []
    for iteration in range(LANCZOS):
        vector = krylov_basis[-1]
        halo_vector = lax.all_to_all(
            pack_rows(vector, send_row), ("rows", "sub"), split_axis=1, concat_axis=1, tiled=True
        )
        near_vector, far_vector = split_product(vector, halo_vector)
        returned_vector = lax.all_to_all(
            far_vector.reshape(DIM, -1), ("rows", "sub"), split_axis=1, concat_axis=1, tiled=True
        )
        image_vec = near_vector + return_rows(returned_vector, send_row, poses_here).reshape(
            1, DIM, poses_here
        )
        image_vec = image_vec - right_product(vector, certificate_mult)
        local_dots = jnp.stack([jnp.sum(member * image_vec) for member in krylov_basis])
        summed_dots, square_total = lax.psum(
            (local_dots, jnp.sum(image_vec * image_vec)), ("rows", "sub")
        )
        projected = summed_dots / entries
        for position in range(len(krylov_basis)):
            image_vec = image_vec - projected[position] * krylov_basis[position]
        beta_now = jnp.sqrt(square_total / entries - jnp.sum(projected * projected) + epsilon)
        krylov_basis.append(image_vec / beta_now)
        alpha_list.append(projected[-1])
        beta_list.append(beta_now)
    tridiagonal = jnp.stack([jnp.stack(alpha_list), jnp.stack(beta_list)])
    return (
        retracted.reshape(RANK * DIM, poses_here),
        krylov_basis[-1].reshape(DIM, poses_here),
        tridiagonal,
    )


def solution(mesh):
    in_specs = (
        P(None, ("rows", "sub")),
        P(None, ("rows", "sub")),
        P(None, ("rows", "sub")),
        P(("rows", "sub"), None),
        P(("rows", "sub"), None),
        P(("rows", "sub")),
        P(("rows", "sub"), None),
    )
    out_specs = (P(None, ("rows", "sub")), P(None, ("rows", "sub")), P())
    return jax.shard_map(
        on_device, mesh=mesh, in_specs=in_specs, out_specs=out_specs, check_vma=False
    )
```

profile of v0, /device:TPU:0, one launch (start us, length us, event | category | flops | bytes accessed | tf_op | source)
XLA Modules:
  0.0 608.0 jit_solution(1578713201348669233)
XLA Ops:
  4.7 7.3 %all-to-all-start = ((f32[32,1,240]{2,1,0:T(1,128)}), f32[32,1,240]{2,1,0:T(1,128)S(1)}, u32[]{:S(2)}, u32[]{:S(2)}) async-start(f32[32,1,240]{2,1,0:T(1,128)} %reshape.1031), calls=%async_computation | async-start | bytes 65536 | tf_op jit(solution)/shard_map/all_to_all | solution.py:103
  14.0 5.5 gather_fusion
  24.2 5.5 gather_fusion.2
  31.8 11.7 %scatter_custom_fusion = f32[15,1536]{0,1:T(8,128)S(1)} fusion(s32[2048]{0:T(1024)S(1)} %bitcast.201, f32[2048,15]{1,0:T(8,128)S(1)} %copy.377, f32[]{:T(128)} %constant.61.clone.1), kind=kCustom, calls=%fused_computation.68 | custom fusion | flops 30720 | bytes 92164 | tf_op jit(solution)/shard_map/scatter-add | solution.py:38
  44.3 5.8 all-to-all-start.1
  51.2 11.7 %scatter_fusion = f32[15,1024]{0,1:T(8,128)S(1)} fusion(f32[15,1024]{0,1:T(8,128)S(1)} %slice-done.1, s32[2048]{0:T(1024)S(1)} %bitcast.183, f32[2048,15]{1,0:T(8,128)S(1)} %copy.378), kind=kCustom, calls=%fused_computation.19 | custom fusion | flops 30720 | bytes 376832 | tf_op jit(solution)/shard_map/scatter-add | solution.py:38
  64.0 2.6 scatter_custom_fusion.2
  67.7 40.7 %all-reduce.4 = (f32[]{:T(128)}, f32[]{:T(128)}) all-reduce(f32[]{:T(128)} %get-tuple-element.95, f32[]{:T(128)} %multiply_reduce_fusion.63), channel_id=1, replica_groups=mesh['rows'=8,'sub'=4] {'rows','sub'}, use_global_device_ids=true, to_apply=%region_10.14 | all-reduce | flops 2 | bytes 16 | tf_op jit(solution)/shard_map/psum | solution.py:115
  113.8 5.5 gather_fusion.6
  122.4 5.5 gather_fusion.3
  130.0 4.9 all-to-all-start.2
  138.5 3.7 all-to-all-done.2
  142.2 2.6 all-to-all-start.4
  146.5 5.5 gather_fusion.5
  154.3 11.8 %scatter_custom_fusion.3 = f32[3,1536]{0,1:T(8,128)S(1)} fusion(s32[2048]{0:T(1024)} %bitcast.202, f32[2048,3]{1,0:T(8,128)S(1)} %copy.389, f32[]{:T(128)} %constant.61.clone.1), kind=kCustom, calls=%fused_computation.64 | custom fusion | flops 6144 | bytes 18944 | tf_op jit(solution)/shard_map/scatter-add | solution.py:38
  167.1 6.4 %all-to-all-start.3 = ((f32[3,32,16]{2,0,1:T(4,128)}), f32[3,32,16]{2,0,1:T(4,128)}, u32[]{:S(2)}, u32[]{:S(2)}) async-start(f32[3,32,16]{2,0,1:T(4,128)} %copy.391), calls=%async_computation.3 | async-start | bytes 131072 | tf_op jit(solution)/shard_map/all_to_all | solution.py:143
  175.9 5.5 gather_fusion.8
  185.8 11.8 %scatter_custom_fusion.6 = f32[15,1536]{0,1:T(8,128)S(1)} fusion(s32[2048]{0:T(1024)} %bitcast.203, f32[2048,15]{1,0:T(8,128)S(1)} %copy.403, f32[]{:T(128)} %constant.61.clone.1), kind=kCustom, calls=%fused_computation.66 | custom fusion | flops 30720 | bytes 92672 | tf_op jit(solution)/shard_map/scatter-add | solution.py:38
  198.5 5.9 all-to-all-start.5
  206.2 11.7 %scatter_fusion.1 = f32[3,1024]{0,1:T(8,128)S(1)} fusion(f32[3,1024]{0,1:T(8,128)S(1)} %slice-done.3, s32[2048]{0:T(1024)S(1)} %bitcast.184, f32[2048,3]{1,0:T(8,128)S(1)} %copy.390), kind=kCustom, calls=%fused_computation.22 | custom fusion | flops 6144 | bytes 81920 | tf_op jit(solution)/shard_map/scatter-add | solution.py:38
  223.0 11.8 %scatter_fusion.2 = f32[15,1024]{0,1:T(8,128)S(1)} fusion(f32[15,1024]{0,1:T(8,128)S(1)} %slice-done, s32[2048]{0:T(1024)S(1)} %bitcast.185, f32[2048,15]{1,0:T(8,128)S(1)} %copy.404), kind=kCustom, calls=%fused_computation.25 | custom fusion | flops 30720 | bytes 376832 | tf_op jit(solution)/shard_map/scatter-add | solution.py:38
  240.8 40.7 %all-reduce.3 = (f32[]{:T(128)}, f32[1]{0:T(128)}) all-reduce(f32[]{:T(128)} %get-tuple-element.72, f32[1]{0:T(128)} %bitcast.41), channel_id=1, replica_groups=mesh['rows'=8,'sub'=4] {'rows','sub'}, use_global_device_ids=true, to_apply=%region_49.56 | all-reduce | flops 2 | bytes 16 | tf_op jit(solution)/shard_map/psum | solution.py:151
  285.9 5.5 gather_fusion.9
  292.4 4.7 all-to-all-start.6
  297.7 6.7 %all-to-all-done.6 = f32[3,32,16]{2,0,1:T(4,128)S(1)} async-done(((f32[3,32,16]{2,0,1:T(4,128)}), f32[3,32,16]{2,0,1:T(4,128)S(1)}, u32[]{:S(2)}, u32[]{:S(2)}) %all-to-all-start.6) | async-done | bytes 6176 | tf_op jit(solution)/shard_map/all_to_all | solution.py:139
  305.3 5.5 gather_fusion.11
  312.5 11.8 %scatter_custom_fusion.9 = f32[3,1536]{0,1:T(8,128)S(1)} fusion(s32[2048]{0:T(1024)} %bitcast.204, f32[2048,3]{1,0:T(8,128)S(1)} %copy.414, f32[]{:T(128)} %constant.61.clone.1), kind=kCustom, calls=%fused_computation.62 | custom fusion | flops 6144 | bytes 18944 | tf_op jit(solution)/shard_map/scatter-add | solution.py:38
  325.2 2.6 all-to-all-start.7
  328.9 11.9 %scatter_fusion.3 = f32[3,1024]{0,1:T(8,128)S(1)} fusion(f32[3,1024]{0,1:T(8,128)S(1)} %slice-done.4, s32[2048]{0:T(1024)S(1)} %bitcast.186, f32[2048,3]{1,0:T(8,128)S(1)} %copy.415), kind=kCustom, calls=%fused_computation.28 | custom fusion | flops 6144 | bytes 81920 | tf_op jit(solution)/shard_map/scatter-add | solution.py:38
  346.0 40.7 %all-reduce.2 = (f32[]{:T(128)}, f32[2]{0:T(128)S(1)}) all-reduce(f32[]{:T(128)} %get-tuple-element.69, f32[2]{0:T(128)S(1)} %pad_maximum_fusion.3), channel_id=1, replica_groups=mesh['rows'=8,'sub'=4] {'rows','sub'}, use_global_device_ids=true, to_apply=%region_62.69 | all-reduce | flops 3 | bytes 24 | tf_op jit(solution)/shard_map/psum | solution.py:151
  392.0 5.5 gather_fusion.12
  398.5 4.7 all-to-all-start.8
  403.9 6.7 %all-to-all-done.8 = f32[3,32,16]{2,0,1:T(4,128)S(1)} async-done(((f32[3,32,16]{2,0,1:T(4,128)}), f32[3,32,16]{2,0,1:T(4,128)S(1)}, u32[]{:S(2)}, u32[]{:S(2)}) %all-to-all-start.8) | async-done | bytes 6176 | tf_op jit(solution)/shard_map/all_to_all | solution.py:139
  411.0 5.5 gather_fusion.14
  417.9 11.8 %scatter_custom_fusion.12 = f32[3,1536]{0,1:T(8,128)S(1)} fusion(s32[2048]{0:T(1024)} %bitcast.205, f32[2048,3]{1,0:T(8,128)S(1)} %copy.428, f32[]{:T(128)} %constant.61.clone.1), kind=kCustom, calls=%fused_computation.60 | custom fusion | flops 6144 | bytes 18944 | tf_op jit(solution)/shard_map/scatter-add | solution.py:38
  430.6 2.6 all-to-all-start.9
  434.2 11.7 %scatter_fusion.4 = f32[3,1024]{0,1:T(8,128)S(1)} fusion(f32[3,1024]{0,1:T(8,128)S(1)} %slice-done.5, s32[2048]{0:T(1024)S(1)} %bitcast.187, f32[2048,3]{1,0:T(8,128)S(1)} %copy.429), kind=kCustom, calls=%fused_computation.31 | custom fusion | flops 6144 | bytes 81920 | tf_op jit(solution)/shard_map/scatter-add | solution.py:38
  446.4 2.8 scatter_custom_fusion.14
  452.0 40.7 %all-reduce.1 = (f32[]{:T(128)}, f32[3]{0:T(128)S(1)}) all-reduce(f32[]{:T(128)} %get-tuple-element.65, f32[3]{0:T(128)S(1)} %pad_maximum_fusion.4), channel_id=1, replica_groups=mesh['rows'=8,'sub'=4] {'rows','sub'}, use_global_device_ids=true, to_apply=%region_77.84 | all-reduce | flops 4 | bytes 32 | tf_op jit(solution)/shard_map/psum | solution.py:151
  498.4 5.5 gather_fusion.15
  504.9 4.6 all-to-all-start.10
  510.2 6.7 %all-to-all-done.10 = f32[3,32,16]{2,0,1:T(4,128)S(1)} async-done(((f32[3,32,16]{2,0,1:T(4,128)}), f32[3,32,16]{2,0,1:T(4,128)S(1)}, u32[]{:S(2)}, u32[]{:S(2)}) %all-to-all-start.10) | async-done | bytes 6176 | tf_op jit(solution)/shard_map/all_to_all | solution.py:139
  517.4 5.5 gather_fusion.17
  524.2 11.8 %scatter_custom_fusion.15 = f32[3,1536]{0,1:T(8,128)S(1)} fusion(s32[2048]{0:T(1024)} %bitcast.206, f32[2048,3]{1,0:T(8,128)S(1)} %copy.442, f32[]{:T(128)} %constant.61.clone.1), kind=kCustom, calls=%fused_computation.58 | custom fusion | flops 6144 | bytes 18944 | tf_op jit(solution)/shard_map/scatter-add | solution.py:38
  536.9 2.6 all-to-all-start.11
  540.6 11.7 %scatter_fusion.5 = f32[3,1024]{0,1:T(8,128)S(1)} fusion(f32[3,1024]{0,1:T(8,128)S(1)} %slice-done.2, s32[2048]{0:T(1024)S(1)} %bitcast.188, f32[2048,3]{1,0:T(8,128)S(1)} %copy.443), kind=kCustom, calls=%fused_computation.34 | custom fusion | flops 6144 | bytes 81920 | tf_op jit(solution)/shard_map/scatter-add | solution.py:38
  558.6 40.7 %all-reduce = (f32[]{:T(128)}, f32[4]{0:T(128)S(1)}) all-reduce(f32[]{:T(128)} %get-tuple-element.60, f32[4]{0:T(128)S(1)} %pad_maximum_fusion.5), channel_id=1, replica_groups=mesh['rows'=8,'sub'=4] {'rows','sub'}, use_global_device_ids=true, to_apply=%region_93.100 | all-reduce | flops 5 | bytes 40 | tf_op jit(solution)/shard_map/psum | solution.py:151
  604.5 3.0 subtract_divide_fusion
  (370 shorter events, 99.4 us)
Async XLA Ops:
  1.4 2.1 copy-start.49
  2.5 118.3 %copy-start.45 = (s32[1024]{0:T(1024)}, s32[1024]{0:T(1024)S(1)}, u32[]{:S(2)}) copy-start(s32[1024]{0:T(1024)S(1)} %pad_clamp_fusion) | copy-start | bytes 12292
  3.7 9.9 %copy-start.34 = (f32[36,2048]{1,0:T(8,128)S(1)}, f32[36,2048]{1,0:T(8,128)}, u32[]{:S(2)}) copy-start(f32[36,2048]{1,0:T(8,128)} %param.21) | copy-start | bytes 884740
  4.7 7.3 %copy-start.6 = (f32[15,1024]{1,0:T(8,128)S(1)}, f32[15,1024]{1,0:T(8,128)}, u32[]{:S(2)}) copy-start(f32[15,1024]{1,0:T(8,128)} %param.19) | copy-start | bytes 184324
  4.7 17.5 %all-to-all-start = ((f32[32,1,240]{2,1,0:T(1,128)}), f32[32,1,240]{2,1,0:T(1,128)S(1)}, u32[]{:S(2)}, u32[]{:S(2)}) async-start(f32[32,1,240]{2,1,0:T(1,128)} %reshape.1031), calls=%async_computation | async-start | bytes 65536 | tf_op jit(solution)/shard_map/all_to_all | solution.py:103
  12.8 101.0 %copy-start.30 = (s32[2048]{0:T(1024)}, s32[2048]{0:T(1024)S(1)}, u32[]{:S(2)}) copy-start(s32[2048]{0:T(1024)S(1)} %fusion.27) | copy-start | bytes 24580
  13.5 6.0 copy-start.41
  13.5 18.3 %copy-start.54 = (s32[2048,1]{0,1:T(1,128)}, s32[2048,1]{0,1:T(1,128)S(1)}, u32[]{:S(2)}) copy-start(s32[2048,1]{0,1:T(1,128)S(1)} %compare_select_fusion.1) | copy-start | bytes 24580
  13.5 10.7 %copy-start.22 = (s32[2048]{0:T(1024)}, s32[2048]{0:T(1024)S(1)}, u32[]{:S(2)}) copy-start(s32[2048]{0:T(1024)S(1)} %fusion.28) | copy-start | bytes 24580
  13.6 16.1 %copy-start.37 = (pred[2048]{0:T(1024)(128)(4,1)}, pred[2048]{0:T(1024)(128)(4,1)S(1)}, u32[]{:S(2)}) copy-start(pred[2048]{0:T(1024)(128)(4,1)S(1)} %compare_and_fusion) | copy-start | bytes 6148
  13.6 37.0 %copy-start.20 = (s32[2048,1]{0,1:T(1,128)}, s32[2048,1]{0,1:T(1,128)S(1)}, u32[]{:S(2)}) copy-start(s32[2048,1]{0,1:T(1,128)S(1)} %compare_select_fusion) | copy-start | bytes 24580
  13.6 50.4 %copy-start.55 = (s32[512,1]{0,1:T(1,128)}, s32[512,1]{0,1:T(1,128)S(1)}, u32[]{:S(2)}) copy-start(s32[512,1]{0,1:T(1,128)S(1)} %compare_select_fusion.4) | copy-start | bytes 6148
  14.0 7.6 %copy-start.11 = (f32[3,3,2048]{2,1,0:T(4,128)}, f32[3,3,2048]{2,1,0:T(4,128)S(1)}, u32[]{:S(2)}) copy-start(f32[3,3,2048]{2,1,0:T(4,128)S(1)} %get-tuple-element.99) | copy-start | bytes 221188
  14.0 7.6 %copy-start.13 = (f32[3,3,2048]{2,1,0:T(4,128)}, f32[3,3,2048]{2,1,0:T(4,128)S(1)}, u32[]{:S(2)}) copy-start(f32[3,3,2048]{2,1,0:T(4,128)S(1)} %get-tuple-element.100) | copy-start | bytes 221188
  14.0 16.4 %copy-start.7 = (f32[3,3,2048]{2,1,0:T(4,128)}, f32[3,3,2048]{2,1,0:T(4,128)S(1)}, u32[]{:S(2)}) copy-start(f32[3,3,2048]{2,1,0:T(4,128)S(1)} %get-tuple-element.97) | copy-start | bytes 221188
  14.0 16.4 %copy-start.9 = (f32[3,3,2048]{2,1,0:T(4,128)}, f32[3,3,2048]{2,1,0:T(4,128)S(1)}, u32[]{:S(2)}) copy-start(f32[3,3,2048]{2,1,0:T(4,128)S(1)} %get-tuple-element.98) | copy-start | bytes 221188
  22.3 9.1 %copy-start.26 = (f32[2048]{0:T(1024)}, f32[2048]{0:T(1024)S(1)}, u32[]{:S(2)}) copy-start(f32[2048]{0:T(1024)S(1)} %fusion.26) | copy-start | bytes 24580
  43.4 6.7 %copy-start.1 = (f32[15,1536]{0,1:T(8,128)}, f32[15,1536]{0,1:T(8,128)S(1)}, u32[]{:S(2)}) copy-start(f32[15,1536]{0,1:T(8,128)S(1)} %scatter_custom_fusion) | copy-start | bytes 276484
  44.3 18.8 %all-to-all-start.1 = ((f32[32,1,240]{2,1,0:T(1,128)}), f32[32,1,240]{2,1,0:T(1,128)S(1)}, u32[]{:S(2)}, u32[]{:S(2)}) async-start(f32[32,1,240]{2,1,0:T(1,128)} %reshape.1033), calls=%async_computation.1 | async-start | bytes 65536 | tf_op jit(solution)/shard_map/all_to_all | solution.py:107
  120.8 1.7 copy-start.31
  127.9 1.1 copy-start.35
  127.9 1.1 copy-start.50
  130.0 12.3 %all-to-all-start.2 = ((f32[3,32,16]{2,0,1:T(4,128)}), f32[3,32,16]{2,0,1:T(4,128)}, u32[]{:S(2)}, u32[]{:S(2)}) async-start(f32[3,32,16]{2,0,1:T(4,128)} %copy.385), calls=%async_computation.2 | async-start | bytes 131072 | tf_op jit(solution)/shard_map/all_to_all | solution.py:139
  134.9 1.1 copy-start.33
  134.9 1.1 copy-start.51
  142.2 24.8 %all-to-all-start.4 = ((f32[32,1,240]{2,1,0:T(1,128)}), f32[32,1,240]{2,1,0:T(1,128)S(1)}, u32[]{:S(2)}, u32[]{:S(2)}) async-start(f32[32,1,240]{2,1,0:T(1,128)} %reshape.1035), calls=%async_computation.4 | async-start | bytes 65536 | tf_op jit(solution)/shard_map/all_to_all | solution.py:120
  146.5 5.5 copy-start.38
  166.1 38.3 %copy-start.3 = (f32[3,1536]{0,1:T(8,128)}, f32[3,1536]{0,1:T(8,128)S(1)}, u32[]{:S(2)}) copy-start(f32[3,1536]{0,1:T(8,128)S(1)} %scatter_custom_fusion.3) | copy-start | bytes 55300
  167.1 31.4 %all-to-all-start.3 = ((f32[3,32,16]{2,0,1:T(4,128)}), f32[3,32,16]{2,0,1:T(4,128)}, u32[]{:S(2)}, u32[]{:S(2)}) async-start(f32[3,32,16]{2,0,1:T(4,128)} %copy.391), calls=%async_computation.3 | async-start | bytes 131072 | tf_op jit(solution)/shard_map/all_to_all | solution.py:143
  175.9 5.5 copy-start.39
  197.5 24.4 %copy-start = (f32[15,1536]{0,1:T(8,128)}, f32[15,1536]{0,1:T(8,128)S(1)}, u32[]{:S(2)}) copy-start(f32[15,1536]{0,1:T(8,128)S(1)} %scatter_custom_fusion.6) | copy-start | bytes 276484
  198.5 36.4 %all-to-all-start.5 = ((f32[32,1,240]{2,1,0:T(1,128)}), f32[32,1,240]{2,1,0:T(1,128)S(1)}, u32[]{:S(2)}, u32[]{:S(2)}) async-start(f32[32,1,240]{2,1,0:T(1,128)} %reshape.1037), calls=%async_computation.5 | async-start | bytes 65536 | tf_op jit(solution)/shard_map/all_to_all | solution.py:124
  221.9 1.1 slice-start
  285.8 5.5 copy-start.52
  292.4 4.7 copy-start.42
  292.4 12.1 %all-to-all-start.6 = ((f32[3,32,16]{2,0,1:T(4,128)}), f32[3,32,16]{2,0,1:T(4,128)S(1)}, u32[]{:S(2)}, u32[]{:S(2)}) async-start(f32[3,32,16]{2,0,1:T(4,128)} %copy.410), calls=%async_computation.6 | async-start | bytes 131072 | tf_op jit(solution)/shard_map/all_to_all | solution.py:139
  305.3 5.5 copy-start.40
  324.3 3.5 copy-start.4
  325.2 15.8 %all-to-all-start.7 = ((f32[3,32,16]{2,0,1:T(4,128)}), f32[3,32,16]{2,0,1:T(4,128)S(1)}, u32[]{:S(2)}, u32[]{:S(2)}) async-start(f32[3,32,16]{2,0,1:T(4,128)} %copy.416), calls=%async_computation.7 | async-start | bytes 131072 | tf_op jit(solution)/shard_map/all_to_all | solution.py:143
  327.8 1.0 slice-start.4
  398.5 12.1 %all-to-all-start.8 = ((f32[3,32,16]{2,0,1:T(4,128)}), f32[3,32,16]{2,0,1:T(4,128)S(1)}, u32[]{:S(2)}, u32[]{:S(2)}) async-start(f32[3,32,16]{2,0,1:T(4,128)} %copy.424), calls=%async_computation.8 | async-start | bytes 131072 | tf_op jit(solution)/shard_map/all_to_all | solution.py:139
  429.7 3.5 copy-start.5
  430.6 15.5 %all-to-all-start.9 = ((f32[3,32,16]{2,0,1:T(4,128)}), f32[3,32,16]{2,0,1:T(4,128)S(1)}, u32[]{:S(2)}, u32[]{:S(2)}) async-start(f32[3,32,16]{2,0,1:T(4,128)} %copy.430), calls=%async_computation.9 | async-start | bytes 131072 | tf_op jit(solution)/shard_map/all_to_all | solution.py:143
  433.2 1.0 slice-start.5
  504.9 12.0 %all-to-all-start.10 = ((f32[3,32,16]{2,0,1:T(4,128)}), f32[3,32,16]{2,0,1:T(4,128)S(1)}, u32[]{:S(2)}, u32[]{:S(2)}) async-start(f32[3,32,16]{2,0,1:T(4,128)} %copy.438), calls=%async_computation.10 | async-start | bytes 131072 | tf_op jit(solution)/shard_map/all_to_all | solution.py:139
  536.0 3.5 copy-start.2
  536.9 15.5 %all-to-all-start.11 = ((f32[3,32,16]{2,0,1:T(4,128)}), f32[3,32,16]{2,0,1:T(4,128)S(1)}, u32[]{:S(2)}, u32[]{:S(2)}) async-start(f32[3,32,16]{2,0,1:T(4,128)} %copy.444), calls=%async_computation.11 | async-start | bytes 131072 | tf_op jit(solution)/shard_map/all_to_all | solution.py:143
  539.5 1.0 slice-start.2
  (26 other events, 21.2 us)
where the time goes:
time: 619 us; the launch traced here: 608 us
  blocking collectives  204 us (33%)
  other arithmetic  195 us (32%)
  local copies, waits for them, and re-layouts  120 us (19%)
  starting transfers between devices  54.6 us (9%)
  waiting for transfers between devices  24 us (4%)
  between operations  11.7 us (2%)
    psum x4, blocking collectives, on_device(): lax.psum((local_dots, jnp.sum(image_vec * image_vec)), ('rows', 'sub'))  163 us
    scatter-add x18, other arithmetic, add_columns(): return total.at[:, index].add(values, mode='drop')  156 us
    gather x18, local copies, waits for them, and re-layouts, take_columns(): return jnp.take(table, index, axis=1, mode='fill', fill_value=0.0)  73 us
    psum x1, blocking collectives, on_device(): total_square = lax.psum(jnp.sum(gradient * gradient), ('rows', 'sub'))  40.7 us
    all_to_all x4, waiting for transfers between devices, on_device(): lax.all_to_all(pack_rows(vector, send_row), ('rows', 'sub'), split_axis=1...  23.9 us
    all_to_all x4, starting transfers between devices, on_device(): lax.all_to_all(pack_rows(vector, send_row), ('rows', 'sub'), split_axis=1...  18.9 us
    unnamed x121, local copies, waits for them, and re-layouts  14.4 us
    all_to_all x4, starting transfers between devices, on_device(): lax.all_to_all(far_vector.reshape(DIM, -1), ('rows', 'sub'), split_axis=1...  14.1 us
  transfers between devices with their start and end apart: 12, of which 4 were waited for; matrix products, arithmetic and copies ran while one was open for 22% of the time, Pallas kernels for 0%

commit v1 on v0

--- a/solution.py
+++ b/solution.py
@@ -149,7 +149,7 @@
         image_vec = image_vec - right_product(vector, certificate_mult)
         local_dots = jnp.stack([jnp.sum(member * image_vec) for member in krylov_basis])
         summed_dots, square_total = lax.psum(
-            (local_dots, jnp.sum(image_vec * image_vec)), ("rows", "sub")
+            lax.psum((local_dots, jnp.sum(image_vec * image_vec)), "sub"), "rows"
         )
         projected = summed_dots / entries
         for position in range(len(krylov_basis)):

time: 619 us -> 570 us (0.921)
  blocking collectives: 204 us -> 160 us
    psum x4 -> x8, blocking collectives: 163 us -> 119 us  [the longest x4 88.8 us: on_device(): lax.psum(lax.psum((local_dots, jnp.sum(image_vec * image_vec)), 'sub'), '...]
  transfers between devices with their start and end apart: 12 -> 12, of which waited for: 4 -> 4; matrix products, arithmetic and copies ran while one was open for 22% -> 24% of each run, Pallas kernels for 0% -> 0%
where the time goes in v1:
time: 570 us; the launch traced here: 559 us
  other arithmetic  194 us (34%)
  blocking collectives  160 us (28%)
  local copies, waits for them, and re-layouts  120 us (21%)
  starting transfers between devices  48.7 us (9%)
  waiting for transfers between devices  23.9 us (4%)
  between operations  12 us (2%)
    scatter-add x18, other arithmetic, add_columns(): return total.at[:, index].add(values, mode='drop')  156 us
    psum x4, blocking collectives, on_device(): lax.psum(lax.psum((local_dots, jnp.sum(image_vec * image_vec)), 'sub'), '...  88.8 us
    gather x18, local copies, waits for them, and re-layouts, take_columns(): return jnp.take(table, index, axis=1, mode='fill', fill_value=0.0)  73 us
    psum x1, blocking collectives, on_device(): total_square = lax.psum(jnp.sum(gradient * gradient), ('rows', 'sub'))  40.7 us
    psum x4, blocking collectives, on_device(): lax.psum((local_dots, jnp.sum(image_vec * image_vec)), 'sub')  30.6 us
    all_to_all x4, waiting for transfers between devices, on_device(): lax.all_to_all(pack_rows(vector, send_row), ('rows', 'sub'), split_axis=1...  23.9 us
    unnamed x121, local copies, waits for them, and re-layouts  14.4 us
    all_to_all x4, starting transfers between devices, on_device(): lax.all_to_all(far_vector.reshape(DIM, -1), ('rows', 'sub'), split_axis=1...  14.1 us
  transfers between devices with their start and end apart: 12, of which 4 were waited for; matrix products, arithmetic and copies ran while one was open for 24% of the time, Pallas kernels for 0%

profile of v1, /device:TPU:0, one launch (start us, length us, event | category | flops | bytes accessed | tf_op | source)
XLA Modules:
  0.0 558.6 jit_solution(11935327352087991550)
XLA Ops:
  4.7 7.3 %all-to-all-start = ((f32[32,1,240]{2,1,0:T(1,128)}), f32[32,1,240]{2,1,0:T(1,128)S(1)}, u32[]{:S(2)}, u32[]{:S(2)}) async-start(f32[32,1,240]{2,1,0:T(1,128)} %reshape.1031), calls=%async_computation | async-start | bytes 65536 | tf_op jit(solution)/shard_map/all_to_all | solution.py:103
  14.0 5.5 gather_fusion
  24.2 5.5 gather_fusion.2
  31.8 11.7 %scatter_custom_fusion = f32[15,1536]{0,1:T(8,128)S(1)} fusion(s32[2048]{0:T(1024)S(1)} %bitcast.201, f32[2048,15]{1,0:T(8,128)S(1)} %copy.377, f32[]{:T(128)} %constant.61.clone.1), kind=kCustom, calls=%fused_computation.68 | custom fusion | flops 30720 | bytes 92164 | tf_op jit(solution)/shard_map/scatter-add | solution.py:38
  44.3 5.8 %all-to-all-start.1 = ((f32[32,1,240]{2,1,0:T(1,128)}), f32[32,1,240]{2,1,0:T(1,128)S(1)}, u32[]{:S(2)}, u32[]{:S(2)}) async-start(f32[32,1,240]{2,1,0:T(1,128)} %reshape.1033), calls=%async_computation.1 | async-start | bytes 65536 | tf_op jit(solution)/shard_map/all_to_all | solution.py:107
  51.2 11.7 %scatter_fusion = f32[15,1024]{0,1:T(8,128)S(1)} fusion(f32[15,1024]{0,1:T(8,128)S(1)} %slice-done.1, s32[2048]{0:T(1024)S(1)} %bitcast.183, f32[2048,15]{1,0:T(8,128)S(1)} %copy.378), kind=kCustom, calls=%fused_computation.19 | custom fusion | flops 30720 | bytes 376832 | tf_op jit(solution)/shard_map/scatter-add | solution.py:38
  64.0 2.6 scatter_custom_fusion.2
  67.7 40.7 %all-reduce = (f32[]{:T(128)}, f32[]{:T(128)}) all-reduce(f32[]{:T(128)} %get-tuple-element.103, f32[]{:T(128)} %multiply_reduce_fusion.63), channel_id=1, replica_groups=mesh['rows'=8,'sub'=4] {'rows','sub'}, use_global_device_ids=true, to_apply=%region_10.14 | all-reduce | flops 2 | bytes 16 | tf_op jit(solution)/shard_map/psum | solution.py:115
  113.8 5.5 gather_fusion.6
  122.4 5.5 gather_fusion.3
  130.0 4.9 all-to-all-start.2
  138.5 3.7 all-to-all-done.2
  142.2 2.6 all-to-all-start.4
  146.5 5.5 gather_fusion.5
  154.3 11.8 %scatter_custom_fusion.3 = f32[3,1536]{0,1:T(8,128)S(1)} fusion(s32[2048]{0:T(1024)} %bitcast.202, f32[2048,3]{1,0:T(8,128)S(1)} %copy.389, f32[]{:T(128)} %constant.61.clone.1), kind=kCustom, calls=%fused_computation.64 | custom fusion | flops 6144 | bytes 18944 | tf_op jit(solution)/shard_map/scatter-add | solution.py:38
  167.0 6.4 %all-to-all-start.3 = ((f32[3,32,16]{2,0,1:T(4,128)}), f32[3,32,16]{2,0,1:T(4,128)}, u32[]{:S(2)}, u32[]{:S(2)}) async-start(f32[3,32,16]{2,0,1:T(4,128)} %copy.391), calls=%async_computation.3 | async-start | bytes 131072 | tf_op jit(solution)/shard_map/all_to_all | solution.py:143
  175.9 5.5 gather_fusion.8
  185.7 11.8 %scatter_custom_fusion.6 = f32[15,1536]{0,1:T(8,128)S(1)} fusion(s32[2048]{0:T(1024)} %bitcast.203, f32[2048,15]{1,0:T(8,128)S(1)} %copy.403, f32[]{:T(128)} %constant.61.clone.1), kind=kCustom, calls=%fused_computation.66 | custom fusion | flops 30720 | bytes 92672 | tf_op jit(solution)/shard_map/scatter-add | solution.py:38
  198.4 5.9 %all-to-all-start.5 = ((f32[32,1,240]{2,1,0:T(1,128)}), f32[32,1,240]{2,1,0:T(1,128)S(1)}, u32[]{:S(2)}, u32[]{:S(2)}) async-start(f32[32,1,240]{2,1,0:T(1,128)} %reshape.1037), calls=%async_computation.5 | async-start | bytes 65536 | tf_op jit(solution)/shard_map/all_to_all | solution.py:124
  206.2 11.7 %scatter_fusion.1 = f32[3,1024]{0,1:T(8,128)S(1)} fusion(f32[3,1024]{0,1:T(8,128)S(1)} %slice-done.3, s32[2048]{0:T(1024)S(1)} %bitcast.184, f32[2048,3]{1,0:T(8,128)S(1)} %copy.390), kind=kCustom, calls=%fused_computation.22 | custom fusion | flops 6144 | bytes 81920 | tf_op jit(solution)/shard_map/scatter-add | solution.py:38
  222.9 11.8 %scatter_fusion.2 = f32[15,1024]{0,1:T(8,128)S(1)} fusion(f32[15,1024]{0,1:T(8,128)S(1)} %slice-done, s32[2048]{0:T(1024)S(1)} %bitcast.185, f32[2048,15]{1,0:T(8,128)S(1)} %copy.404), kind=kCustom, calls=%fused_computation.25 | custom fusion | flops 30720 | bytes 376832 | tf_op jit(solution)/shard_map/scatter-add | solution.py:38
  240.8 7.7 %all-reduce.8 = (f32[]{:T(128)}, f32[1]{0:T(128)}) all-reduce(f32[]{:T(128)} %get-tuple-element.72, f32[1]{0:T(128)} %bitcast.41), channel_id=1, replica_groups=mesh['rows'=8,'sub'=4] {'sub'}, use_global_device_ids=true, to_apply=%region_50.57 | all-reduce | flops 2 | bytes 16 | tf_op jit(solution)/shard_map/psum | solution.py:152
  248.5 22.0 %all-reduce.4 = (f32[]{:T(128)}, f32[1]{0:T(128)}) all-reduce(f32[]{:T(128)} %get-tuple-element.89, f32[1]{0:T(128)} %get-tuple-element.90), channel_id=1, replica_groups=mesh['rows'=8,'sub'=4] {'rows'}, use_global_device_ids=true, to_apply=%region_51.58 | all-reduce | flops 2 | bytes 16 | tf_op jit(solution)/shard_map/psum | solution.py:151
  274.9 5.5 gather_fusion.9
  281.4 2.7 all-to-all-start.6
  284.8 6.7 %all-to-all-done.6 = f32[3,32,16]{2,0,1:T(4,128)S(1)} async-done(((f32[3,32,16]{2,0,1:T(4,128)}), f32[3,32,16]{2,0,1:T(4,128)S(1)}, u32[]{:S(2)}, u32[]{:S(2)}) %all-to-all-start.6) | async-done | bytes 6176 | tf_op jit(solution)/shard_map/all_to_all | solution.py:139
  292.3 5.5 gather_fusion.11
  299.6 11.8 %scatter_custom_fusion.9 = f32[3,1536]{0,1:T(8,128)S(1)} fusion(s32[2048]{0:T(1024)} %bitcast.204, f32[2048,3]{1,0:T(8,128)S(1)} %copy.414, f32[]{:T(128)} %constant.61.clone.1), kind=kCustom, calls=%fused_computation.62 | custom fusion | flops 6144 | bytes 18944 | tf_op jit(solution)/shard_map/scatter-add | solution.py:38
  316.0 11.7 %scatter_fusion.3 = f32[3,1024]{0,1:T(8,128)S(1)} fusion(f32[3,1024]{0,1:T(8,128)S(1)} %slice-done.4, s32[2048]{0:T(1024)S(1)} %bitcast.186, f32[2048,3]{1,0:T(8,128)S(1)} %copy.415), kind=kCustom, calls=%fused_computation.28 | custom fusion | flops 6144 | bytes 81920 | tf_op jit(solution)/shard_map/scatter-add | solution.py:38
  332.9 7.7 %all-reduce.7 = (f32[]{:T(128)}, f32[2]{0:T(128)S(1)}) all-reduce(f32[]{:T(128)} %get-tuple-element.69, f32[2]{0:T(128)S(1)} %pad_maximum_fusion.3), channel_id=1, replica_groups=mesh['rows'=8,'sub'=4] {'sub'}, use_global_device_ids=true, to_apply=%region_65.72 | all-reduce | flops 3 | bytes 24 | tf_op jit(solution)/shard_map/psum | solution.py:152
  340.6 22.4 %all-reduce.3 = (f32[]{:T(128)}, f32[2]{0:T(128)S(1)}) all-reduce(f32[]{:T(128)} %get-tuple-element.87, f32[2]{0:T(128)S(1)} %get-tuple-element.88), channel_id=1, replica_groups=mesh['rows'=8,'sub'=4] {'rows'}, use_global_device_ids=true, to_apply=%region_66.73 | all-reduce | flops 3 | bytes 24 | tf_op jit(solution)/shard_map/psum | solution.py:151
  368.3 5.5 gather_fusion.12
  374.8 2.6 all-to-all-start.8
  378.0 6.7 %all-to-all-done.8 = f32[3,32,16]{2,0,1:T(4,128)S(1)} async-done(((f32[3,32,16]{2,0,1:T(4,128)}), f32[3,32,16]{2,0,1:T(4,128)S(1)}, u32[]{:S(2)}, u32[]{:S(2)}) %all-to-all-start.8) | async-done | bytes 6176 | tf_op jit(solution)/shard_map/all_to_all | solution.py:139
  385.2 5.5 gather_fusion.14
  392.0 11.8 %scatter_custom_fusion.12 = f32[3,1536]{0,1:T(8,128)S(1)} fusion(s32[2048]{0:T(1024)} %bitcast.205, f32[2048,3]{1,0:T(8,128)S(1)} %copy.428, f32[]{:T(128)} %constant.61.clone.1), kind=kCustom, calls=%fused_computation.60 | custom fusion | flops 6144 | bytes 18944 | tf_op jit(solution)/shard_map/scatter-add | solution.py:38
  408.4 11.7 %scatter_fusion.4 = f32[3,1024]{0,1:T(8,128)S(1)} fusion(f32[3,1024]{0,1:T(8,128)S(1)} %slice-done.5, s32[2048]{0:T(1024)S(1)} %bitcast.187, f32[2048,3]{1,0:T(8,128)S(1)} %copy.429), kind=kCustom, calls=%fused_computation.31 | custom fusion | flops 6144 | bytes 81920 | tf_op jit(solution)/shard_map/scatter-add | solution.py:38
  425.9 7.6 %all-reduce.6 = (f32[]{:T(128)}, f32[3]{0:T(128)S(1)}) all-reduce(f32[]{:T(128)} %get-tuple-element.65, f32[3]{0:T(128)S(1)} %pad_maximum_fusion.4), channel_id=1, replica_groups=mesh['rows'=8,'sub'=4] {'sub'}, use_global_device_ids=true, to_apply=%region_82.89 | all-reduce | flops 4 | bytes 32 | tf_op jit(solution)/shard_map/psum | solution.py:152
  433.5 22.2 %all-reduce.2 = (f32[]{:T(128)}, f32[3]{0:T(128)S(1)}) all-reduce(f32[]{:T(128)} %get-tuple-element.85, f32[3]{0:T(128)S(1)} %get-tuple-element.86), channel_id=1, replica_groups=mesh['rows'=8,'sub'=4] {'rows'}, use_global_device_ids=true, to_apply=%region_83.90 | all-reduce | flops 4 | bytes 32 | tf_op jit(solution)/shard_map/psum | solution.py:151
  461.6 5.5 gather_fusion.15
  468.1 2.8 all-to-all-start.10
  471.6 6.7 %all-to-all-done.10 = f32[3,32,16]{2,0,1:T(4,128)S(1)} async-done(((f32[3,32,16]{2,0,1:T(4,128)}), f32[3,32,16]{2,0,1:T(4,128)S(1)}, u32[]{:S(2)}, u32[]{:S(2)}) %all-to-all-start.10) | async-done | bytes 6176 | tf_op jit(solution)/shard_map/all_to_all | solution.py:139
  478.7 5.5 gather_fusion.17
  485.6 11.8 %scatter_custom_fusion.15 = f32[3,1536]{0,1:T(8,128)S(1)} fusion(s32[2048]{0:T(1024)} %bitcast.206, f32[2048,3]{1,0:T(8,128)S(1)} %copy.442, f32[]{:T(128)} %constant.61.clone.1), kind=kCustom, calls=%fused_computation.58 | custom fusion | flops 6144 | bytes 18944 | tf_op jit(solution)/shard_map/scatter-add | solution.py:38
  501.9 11.7 %scatter_fusion.5 = f32[3,1024]{0,1:T(8,128)S(1)} fusion(f32[3,1024]{0,1:T(8,128)S(1)} %slice-done.2, s32[2048]{0:T(1024)S(1)} %bitcast.188, f32[2048,3]{1,0:T(8,128)S(1)} %copy.443), kind=kCustom, calls=%fused_computation.34 | custom fusion | flops 6144 | bytes 81920 | tf_op jit(solution)/shard_map/scatter-add | solution.py:38
  520.0 7.6 %all-reduce.5 = (f32[]{:T(128)}, f32[4]{0:T(128)S(1)}) all-reduce(f32[]{:T(128)} %get-tuple-element.60, f32[4]{0:T(128)S(1)} %pad_maximum_fusion.5), channel_id=1, replica_groups=mesh['rows'=8,'sub'=4] {'sub'}, use_global_device_ids=true, to_apply=%region_100.107 | all-reduce | flops 5 | bytes 40 | tf_op jit(solution)/shard_map/psum | solution.py:152
  527.6 22.2 %all-reduce.1 = (f32[]{:T(128)}, f32[4]{0:T(128)S(1)}) all-reduce(f32[]{:T(128)} %get-tuple-element.83, f32[4]{0:T(128)S(1)} %get-tuple-element.84), channel_id=1, replica_groups=mesh['rows'=8,'sub'=4] {'rows'}, use_global_device_ids=true, to_apply=%region_101.108 | all-reduce | flops 5 | bytes 40 | tf_op jit(solution)/shard_map/psum | solution.py:151
  555.1 3.0 subtract_divide_fusion
  (374 shorter events, 109.5 us)
Async XLA Ops:
  1.4 2.1 copy-start.49
  2.5 118.3 %copy-start.45 = (s32[1024]{0:T(1024)}, s32[1024]{0:T(1024)S(1)}, u32[]{:S(2)}) copy-start(s32[1024]{0:T(1024)S(1)} %pad_clamp_fusion) | copy-start | bytes 12292
  3.7 9.9 %copy-start.34 = (f32[36,2048]{1,0:T(8,128)S(1)}, f32[36,2048]{1,0:T(8,128)}, u32[]{:S(2)}) copy-start(f32[36,2048]{1,0:T(8,128)} %param.21) | copy-start | bytes 884740
  4.7 7.3 %copy-start.6 = (f32[15,1024]{1,0:T(8,128)S(1)}, f32[15,1024]{1,0:T(8,128)}, u32[]{:S(2)}) copy-start(f32[15,1024]{1,0:T(8,128)} %param.19) | copy-start | bytes 184324
  4.7 17.5 %all-to-all-start = ((f32[32,1,240]{2,1,0:T(1,128)}), f32[32,1,240]{2,1,0:T(1,128)S(1)}, u32[]{:S(2)}, u32[]{:S(2)}) async-start(f32[32,1,240]{2,1,0:T(1,128)} %reshape.1031), calls=%async_computation | async-start | bytes 65536 | tf_op jit(solution)/shard_map/all_to_all | solution.py:103
  12.8 101.0 %copy-start.30 = (s32[2048]{0:T(1024)}, s32[2048]{0:T(1024)S(1)}, u32[]{:S(2)}) copy-start(s32[2048]{0:T(1024)S(1)} %fusion.27) | copy-start | bytes 24580
  13.5 6.0 %copy-start.41 = (pred[2048]{0:T(1024)(128)(4,1)}, pred[2048]{0:T(1024)(128)(4,1)S(1)}, u32[]{:S(2)}) copy-start(pred[2048]{0:T(1024)(128)(4,1)S(1)} %compare_and_fusion.1) | copy-start | bytes 6148
  13.5 18.3 %copy-start.54 = (s32[2048,1]{0,1:T(1,128)}, s32[2048,1]{0,1:T(1,128)S(1)}, u32[]{:S(2)}) copy-start(s32[2048,1]{0,1:T(1,128)S(1)} %compare_select_fusion.1) | copy-start | bytes 24580
  13.5 10.7 %copy-start.22 = (s32[2048]{0:T(1024)}, s32[2048]{0:T(1024)S(1)}, u32[]{:S(2)}) copy-start(s32[2048]{0:T(1024)S(1)} %fusion.28) | copy-start | bytes 24580
  13.6 16.1 %copy-start.37 = (pred[2048]{0:T(1024)(128)(4,1)}, pred[2048]{0:T(1024)(128)(4,1)S(1)}, u32[]{:S(2)}) copy-start(pred[2048]{0:T(1024)(128)(4,1)S(1)} %compare_and_fusion) | copy-start | bytes 6148
  13.6 37.0 %copy-start.20 = (s32[2048,1]{0,1:T(1,128)}, s32[2048,1]{0,1:T(1,128)S(1)}, u32[]{:S(2)}) copy-start(s32[2048,1]{0,1:T(1,128)S(1)} %compare_select_fusion) | copy-start | bytes 24580
  13.6 50.4 %copy-start.55 = (s32[512,1]{0,1:T(1,128)}, s32[512,1]{0,1:T(1,128)S(1)}, u32[]{:S(2)}) copy-start(s32[512,1]{0,1:T(1,128)S(1)} %compare_select_fusion.4) | copy-start | bytes 6148
  14.0 7.6 %copy-start.11 = (f32[3,3,2048]{2,1,0:T(4,128)}, f32[3,3,2048]{2,1,0:T(4,128)S(1)}, u32[]{:S(2)}) copy-start(f32[3,3,2048]{2,1,0:T(4,128)S(1)} %get-tuple-element.107) | copy-start | bytes 221188
  14.0 7.6 %copy-start.13 = (f32[3,3,2048]{2,1,0:T(4,128)}, f32[3,3,2048]{2,1,0:T(4,128)S(1)}, u32[]{:S(2)}) copy-start(f32[3,3,2048]{2,1,0:T(4,128)S(1)} %get-tuple-element.108) | copy-start | bytes 221188
  14.0 16.4 %copy-start.7 = (f32[3,3,2048]{2,1,0:T(4,128)}, f32[3,3,2048]{2,1,0:T(4,128)S(1)}, u32[]{:S(2)}) copy-start(f32[3,3,2048]{2,1,0:T(4,128)S(1)} %get-tuple-element.105) | copy-start | bytes 221188
  14.0 16.4 %copy-start.9 = (f32[3,3,2048]{2,1,0:T(4,128)}, f32[3,3,2048]{2,1,0:T(4,128)S(1)}, u32[]{:S(2)}) copy-start(f32[3,3,2048]{2,1,0:T(4,128)S(1)} %get-tuple-element.106) | copy-start | bytes 221188
  22.3 9.1 %copy-start.26 = (f32[2048]{0:T(1024)}, f32[2048]{0:T(1024)S(1)}, u32[]{:S(2)}) copy-start(f32[2048]{0:T(1024)S(1)} %fusion.26) | copy-start | bytes 24580
  43.4 6.7 %copy-start.1 = (f32[15,1536]{0,1:T(8,128)}, f32[15,1536]{0,1:T(8,128)S(1)}, u32[]{:S(2)}) copy-start(f32[15,1536]{0,1:T(8,128)S(1)} %scatter_custom_fusion) | copy-start | bytes 276484
  44.3 18.8 %all-to-all-start.1 = ((f32[32,1,240]{2,1,0:T(1,128)}), f32[32,1,240]{2,1,0:T(1,128)S(1)}, u32[]{:S(2)}, u32[]{:S(2)}) async-start(f32[32,1,240]{2,1,0:T(1,128)} %reshape.1033), calls=%async_computation.1 | async-start | bytes 65536 | tf_op jit(solution)/shard_map/all_to_all | solution.py:107
  120.8 1.7 copy-start.31
  127.9 1.1 copy-start.35
  127.9 1.1 copy-start.50
  130.0 12.3 %all-to-all-start.2 = ((f32[3,32,16]{2,0,1:T(4,128)}), f32[3,32,16]{2,0,1:T(4,128)}, u32[]{:S(2)}, u32[]{:S(2)}) async-start(f32[3,32,16]{2,0,1:T(4,128)} %copy.385), calls=%async_computation.2 | async-start | bytes 131072 | tf_op jit(solution)/shard_map/all_to_all | solution.py:139
  134.8 1.1 copy-start.33
  134.9 1.1 copy-start.51
  142.2 24.8 %all-to-all-start.4 = ((f32[32,1,240]{2,1,0:T(1,128)}), f32[32,1,240]{2,1,0:T(1,128)S(1)}, u32[]{:S(2)}, u32[]{:S(2)}) async-start(f32[32,1,240]{2,1,0:T(1,128)} %reshape.1035), calls=%async_computation.4 | async-start | bytes 65536 | tf_op jit(solution)/shard_map/all_to_all | solution.py:120
  146.5 5.5 copy-start.38
  166.1 38.3 %copy-start.3 = (f32[3,1536]{0,1:T(8,128)}, f32[3,1536]{0,1:T(8,128)S(1)}, u32[]{:S(2)}) copy-start(f32[3,1536]{0,1:T(8,128)S(1)} %scatter_custom_fusion.3) | copy-start | bytes 55300
  167.0 31.4 %all-to-all-start.3 = ((f32[3,32,16]{2,0,1:T(4,128)}), f32[3,32,16]{2,0,1:T(4,128)}, u32[]{:S(2)}, u32[]{:S(2)}) async-start(f32[3,32,16]{2,0,1:T(4,128)} %copy.391), calls=%async_computation.3 | async-start | bytes 131072 | tf_op jit(solution)/shard_map/all_to_all | solution.py:143
  175.9 5.5 copy-start.39
  197.5 24.4 %copy-start = (f32[15,1536]{0,1:T(8,128)}, f32[15,1536]{0,1:T(8,128)S(1)}, u32[]{:S(2)}) copy-start(f32[15,1536]{0,1:T(8,128)S(1)} %scatter_custom_fusion.6) | copy-start | bytes 276484
  198.4 36.4 %all-to-all-start.5 = ((f32[32,1,240]{2,1,0:T(1,128)}), f32[32,1,240]{2,1,0:T(1,128)S(1)}, u32[]{:S(2)}, u32[]{:S(2)}) async-start(f32[32,1,240]{2,1,0:T(1,128)} %reshape.1037), calls=%async_computation.5 | async-start | bytes 65536 | tf_op jit(solution)/shard_map/all_to_all | solution.py:124
  221.9 1.1 slice-start
  274.9 5.5 copy-start.52
  281.4 2.7 copy-start.42
  281.4 10.1 %all-to-all-start.6 = ((f32[3,32,16]{2,0,1:T(4,128)}), f32[3,32,16]{2,0,1:T(4,128)S(1)}, u32[]{:S(2)}, u32[]{:S(2)}) async-start(f32[3,32,16]{2,0,1:T(4,128)} %copy.410), calls=%async_computation.6 | async-start | bytes 131072 | tf_op jit(solution)/shard_map/all_to_all | solution.py:139
  292.3 5.5 copy-start.40
  311.4 3.5 copy-start.4
  312.3 15.5 %all-to-all-start.7 = ((f32[3,32,16]{2,0,1:T(4,128)}), f32[3,32,16]{2,0,1:T(4,128)S(1)}, u32[]{:S(2)}, u32[]{:S(2)}) async-start(f32[3,32,16]{2,0,1:T(4,128)} %copy.416), calls=%async_computation.7 | async-start | bytes 131072 | tf_op jit(solution)/shard_map/all_to_all | solution.py:143
  314.9 1.0 slice-start.4
  374.8 10.0 %all-to-all-start.8 = ((f32[3,32,16]{2,0,1:T(4,128)}), f32[3,32,16]{2,0,1:T(4,128)S(1)}, u32[]{:S(2)}, u32[]{:S(2)}) async-start(f32[3,32,16]{2,0,1:T(4,128)} %copy.424), calls=%async_computation.8 | async-start | bytes 131072 | tf_op jit(solution)/shard_map/all_to_all | solution.py:139
  403.8 3.5 copy-start.5
  404.7 15.5 %all-to-all-start.9 = ((f32[3,32,16]{2,0,1:T(4,128)}), f32[3,32,16]{2,0,1:T(4,128)S(1)}, u32[]{:S(2)}, u32[]{:S(2)}) async-start(f32[3,32,16]{2,0,1:T(4,128)} %copy.430), calls=%async_computation.9 | async-start | bytes 131072 | tf_op jit(solution)/shard_map/all_to_all | solution.py:143
  407.4 1.0 slice-start.5
  468.1 10.2 %all-to-all-start.10 = ((f32[3,32,16]{2,0,1:T(4,128)}), f32[3,32,16]{2,0,1:T(4,128)S(1)}, u32[]{:S(2)}, u32[]{:S(2)}) async-start(f32[3,32,16]{2,0,1:T(4,128)} %copy.438), calls=%async_computation.10 | async-start | bytes 131072 | tf_op jit(solution)/shard_map/all_to_all | solution.py:139
  497.3 3.5 copy-start.2
  498.3 15.5 %all-to-all-start.11 = ((f32[3,32,16]{2,0,1:T(4,128)}), f32[3,32,16]{2,0,1:T(4,128)S(1)}, u32[]{:S(2)}, u32[]{:S(2)}) async-start(f32[3,32,16]{2,0,1:T(4,128)} %copy.444), calls=%async_computation.11 | async-start | bytes 131072 | tf_op jit(solution)/shard_map/all_to_all | solution.py:143
  500.9 1.0 slice-start.2
  (26 other events, 21.2 us)
